TPU v7x, 8 devices: a whole 2x2x1 slice. The times are simulated.
8 devices in a mesh: dp: 1 (over z), tp: 2 (over y), sp: 4 (over x, core).
Axes of the slice: x: 2, y: 2, z: 1, core: 2. Of those that a mesh axis runs over, the one named last changes fastest.
Arguments:
- tok_hidden: bfloat16 [256, 2048], P('dp')
- cache_len: int32 [256], P('dp')
- k_cache: bfloat16 [256, 32, 64, 64], P('dp', 'tp', 'sp')
- v_cache: bfloat16 [256, 32, 64, 64], P('dp', 'tp', 'sp')
- ln_gain: float32 [2048], replicated
- ln_bias: float32 [2048], replicated
- w_qkv: bfloat16 [2048, 3, 32, 64], P(None, None, 'tp')
- b_qkv: bfloat16 [3, 32, 64], P(None, 'tp')
- w_out: bfloat16 [32, 64, 2048], P('tp')
- b_out: bfloat16 [2048], replicated
Outputs:
- output 1: bfloat16 [256, 2048], P('dp')
- output 2: bfloat16 [256, 32, 64, 64], P('dp', 'tp', 'sp')
- output 3: bfloat16 [256, 32, 64, 64], P('dp', 'tp', 'sp')
All inputs are finite; a program needn't handle non-finite values.
Results may differ from a plain program's by a relative error of at most 0.00850116.
Values sent between devices are 32-bit elements.
A program may use at most 1 GiB of HBM per device.

v0:
```python
import jax
import jax.numpy as jnp
from jax import lax
from jax.sharding import PartitionSpec as P, NamedSharding


def norm_project(tok_hidden, ln_gain, ln_bias, w_qkv, b_qkv):
    x_f32 = tok_hidden.astype(jnp.float32)
    mean_x = jnp.mean(x_f32, axis=-1, keepdims=True)
    centered = x_f32 - mean_x
    var_x = jnp.mean(centered * centered, axis=-1, keepdims=True)
    hidden = (centered * lax.rsqrt(var_x + 1e-5) * ln_gain + ln_bias).astype(jnp.bfloat16)
    qkv_all = jnp.einsum('bm,mthd->bthd', hidden, w_qkv, preferred_element_type=jnp.float32)
    qkv_all = (qkv_all + b_qkv.astype(jnp.float32)).astype(jnp.bfloat16)
    return x_f32, qkv_all[:, 0], qkv_all[:, 1], qkv_all[:, 2]


def write_token(cache, new_row, local_len):
    slots = jnp.arange(cache.shape[2], dtype=jnp.int32)
    write_mask = (slots[None, :] == local_len[:, None])[:, None, :, None]
    return jnp.where(write_mask, new_row[:, :, None, :], cache)


def solution(mesh):
    cache_spec = P('dp', 'tp', 'sp', None)
    row_spec = P('dp', None)

    def local_block(tok_hidden, cache_len, k_cache, v_cache, ln_gain, ln_bias, w_qkv, b_qkv, w_out, b_out):
        head_dim = k_cache.shape[3]
        seq_local = k_cache.shape[2]
        x_f32, q_new, k_new, v_new = norm_project(tok_hidden, ln_gain, ln_bias, w_qkv, b_qkv)
        local_len = cache_len - lax.axis_index('sp') * seq_local
        k_out = write_token(k_cache, k_new, local_len)
        v_out = write_token(v_cache, v_new, local_len)
        slots = jnp.arange(seq_local, dtype=jnp.int32)
        scores = jnp.einsum('bhd,bhsd->bhs', q_new, k_out, preferred_element_type=jnp.float32) * head_dim ** -0.5
        valid = (slots[None, :] <= local_len[:, None])[:, None, :]
        masked = jnp.where(valid, scores, -1e30)
        local_max = jnp.max(masked, axis=-1)
        weights = jnp.where(valid, jnp.exp(masked - local_max[..., None]), 0.0)
        local_sum = jnp.sum(weights, axis=-1)
        local_acc = jnp.einsum('bhs,bhsd->bhd', weights.astype(jnp.bfloat16), v_out, preferred_element_type=jnp.float32)
        global_max = lax.pmax(local_max, 'sp')
        factor = jnp.exp(local_max - global_max)
        combined_in = jnp.concatenate([local_acc * factor[..., None], (local_sum * factor)[..., None]], axis=-1)
        totals = lax.psum(combined_in, 'sp')
        attended = (totals[..., :head_dim] / totals[..., head_dim:]).astype(jnp.bfloat16)
        partial_out = jnp.einsum('bhd,hdm->bm', attended, w_out, preferred_element_type=jnp.float32)
        projected = lax.psum(partial_out, 'tp')
        y_out = (x_f32 + projected + b_out.astype(jnp.float32)).astype(jnp.bfloat16)
        return y_out, k_out, v_out

    return jax.shard_map(
        local_block,
        mesh=mesh,
        in_specs=(row_spec, P('dp'), cache_spec, cache_spec, P(None), P(None), P(None, None, 'tp', None), P(None, 'tp', None), P('tp', None, None), P(None)),
        out_specs=(row_spec, cache_spec, cache_spec),
        check_vma=False,
    )
```

profile of v0, /device:TPU:0, one launch (start us, length us, event | category | flops | bytes accessed | tf_op | source)
XLA Modules:
  0.0 160.5 jit_solution(4095460325357645621)
XLA Ops:
  7.2 0.0 copy-start
  7.2 0.0 copy-start.1
  7.2 0.0 copy-start.5
  7.2 0.0 copy-start.4
  7.2 0.0 all-reduce.3.cloned.1.call-start
  7.3 1.5 convert_reduce_fusion
  8.8 1.6 %fusion.2 = f32[256]{0:T(256)S(1)} fusion(bf16[256,2048]{1,0:T(8,128)(2,1)} %param.10, f32[256]{0:T(256)S(1)} %broadcast_multiply_fusion.1), kind=kLoop, calls=%fused_computation.11 | loop fusion | flops 2096896 | bytes 1050624 | tf_op jit(solution)/shard_map/reduce_sum | solution.py:11
  10.4 0.0 copy-done.1
  10.5 0.0 copy-done
  10.5 0.0 copy-done.5
  10.5 0.0 copy-done.4
  10.5 6.9 %fusion.8 = f32[256,3072]{0,1:S(1)} fusion(bf16[2048,3072]{0,1:T(8,128)(2,1)} %bitcast.23, bf16[256,2048]{1,0:T(8,128)(2,1)S(1)} %copy-done, f32[2048]{0:T(1024)S(1)} %copy-done.4, f32[2048]{0:T(1024)S(1)} %copy-done.5, f32[256]{0:T(256)S(1)} %add_rsqrt_fusion, f32[256]{0:T(256)S(1)} %broadcast_multiply_fusion.1), kind=kOutput, calls=%fused_computation.18 | convolution fusion | flops 3224371200 | bytes 16795648
  17.4 0.5 add_convert_fusion
  17.9 0.0 copy-start.3
  17.9 0.2 slice_bitcast_fusion
  18.1 0.5 copy-done.3
  18.6 11.3 %multiply_reduce_fusion.1 = (f32[256,16,16]{0,2,1:T(8,128)S(1)}, bf16[256,16,16,64]{0,3,2,1:T(8,128)(2,1)}) fusion(f32[256,16,64]{0,2,1:T(8,128)S(1)} %get-tuple-element.11, bf16[256,16,16,64]{0,3,2,1:T(8,128)(2,1)} %param.12, bf16[256,16,64]{0,2,1:T(8,128)(2,1)S(1)} %get-tuple-element.10, pred[256,16]{0,1:T(8,128)(4,1)S(1)} %get-tuple-element.15), kind=kLoop, calls=%fused_computation.1 | loop fusion | flops 16711680 | bytes 18616320 | tf_op jit(solution)/shard_map/bhd,bhsd->bhs/dot_general | solution.py:36
  29.9 0.1 fusion.18
  29.9 0.1 fusion.21
  30.0 13.1 %pmax.7 = f32[256,16]{0,1:T(8,128)S(1)} all-reduce(f32[256,16]{0,1:T(8,128)S(1)} %fusion.18), channel_id=1, replica_groups=mesh['dp'=1,'tp'=2,'sp'=4] {'sp'}, use_global_device_ids=true, to_apply=%region_3.4 | all-reduce | flops 4096 | bytes 32768 | tf_op jit(solution)/shard_map/pmax | solution.py:43
  43.1 10.8 %multiply_reduce_fusion = (f32[256,16,64]{0,2,1:T(8,128)S(1)}, bf16[256,16,16,64]{0,3,2,1:T(8,128)(2,1)}) fusion(f32[256,16,16]{0,2,1:T(8,128)S(1)} %get-tuple-element.12, bf16[256,16,16,64]{0,3,2,1:T(8,128)(2,1)} %param.13, bf16[256,16,64]{0,2,1:T(8,128)(2,1)S(1)} %get-tuple-element.9, pred[256,16]{0,1:T(8,128)(4,1)S(1)} %get-tuple-element.15), kind=kLoop, calls=%fused_computation | loop fusion | flops 16515072 | bytes 18616320 | tf_op jit(solution)/shard_map/bhs,bhsd->bhd/dot_general | solution.py:42
  53.9 0.1 broadcast_multiply_fusion
  54.0 1.1 pad_maximum_fusion
  55.1 0.0 all-reduce.3.cloned.1.call-update
  55.1 0.0 all-reduce.5.cloned.1.call-start
  55.2 32.1 %all-reduce.3.cloned.1.call-done = f32[256,16,65]{0,2,1:T(8,128)} async-done(((f32[256,16,65]{0,2,1:T(8,128)}), f32[256,16,65]{0,2,1:T(8,128)}) %all-reduce.3.cloned.1.call-update) | async-done | bytes 1064976 | tf_op jit(solution)/shard_map/psum | solution.py:46
  87.2 0.9 slice.24
  88.2 5.1 %convolution_bitcast_fusion = f32[256,2048]{1,0:T(8,128)} fusion(bf16[16,64,2048]{2,1,0:T(8,128)(2,1)} %param.18, f32[256,16,65]{0,2,1:T(8,128)} %all-reduce.3.cloned.1.call-done, f32[256,16]{0,1:T(8,128)S(1)} %bitcast.22), kind=kOutput, calls=%fused_computation.8 | convolution fusion | flops 1074266112 | bytes 7356416 | tf_op jit(solution)/shard_map/bhd,hdm->bm/dot_general | solution.py:48
  93.3 0.0 copy-start.2
  93.3 0.0 all-reduce.5.cloned.1.call-update
  93.3 0.7 copy-done.2
  94.0 56.8 %all-reduce.5.cloned.1.call-done = f32[256,2048]{1,0:T(8,128)} async-done(((f32[256,2048]{1,0:T(8,128)}), f32[256,2048]{1,0:T(8,128)}) %all-reduce.5.cloned.1.call-update) | async-done | bytes 2097168 | tf_op jit(solution)/shard_map/psum | solution.py:49
  150.8 2.9 %fusion.7 = bf16[256,2048]{1,0:T(8,128)(2,1)} fusion(f32[256,2048]{1,0:T(8,128)} %all-reduce.5.cloned.1.call-done, bf16[256,2048]{1,0:T(8,128)(2,1)S(1)} %copy-done, f32[2048]{0:T(1024)S(1)} %convert_element_type.30), kind=kLoop, calls=%fused_computation.16 | loop fusion | flops 2097152 | bytes 4202496 | tf_op jit(solution)/shard_map/convert_element_type | solution.py:50
  (9 shorter events, 0.1 us)
Async XLA Ops:
  7.2 3.3 %copy-start = (bf16[256,2048]{1,0:T(8,128)(2,1)S(1)}, bf16[256,2048]{1,0:T(8,128)(2,1)}, u32[]{:S(2)}) copy-start(bf16[256,2048]{1,0:T(8,128)(2,1)} %param.10) | copy-start | bytes 3145732
  7.2 3.3 %copy-start.1 = (bf16[3,16,64]{2,1,0:T(8,128)(2,1)S(1)}, bf16[3,16,64]{2,1,0:T(8,128)(2,1)}, u32[]{:S(2)}) copy-start(bf16[3,16,64]{2,1,0:T(8,128)(2,1)} %param.17) | copy-start | bytes 18436
  7.2 3.3 %copy-start.5 = (f32[2048]{0:T(1024)S(1)}, f32[2048]{0:T(1024)}, u32[]{:S(2)}) copy-start(f32[2048]{0:T(1024)} %param.14) | copy-start | bytes 24580
  7.2 3.3 %copy-start.4 = (f32[2048]{0:T(1024)S(1)}, f32[2048]{0:T(1024)}, u32[]{:S(2)}) copy-start(f32[2048]{0:T(1024)} %param.15) | copy-start | bytes 24580
  7.2 80.0 %all-reduce.3.cloned.1.call-start = ((), (), s32[]{:S(2)}) async-start(), calls=%async_computation | async-start | bytes 2359296 | tf_op jit(solution)/shard_map/psum | solution.py:46
  17.9 0.7 copy-start.3
  55.1 95.6 %all-reduce.5.cloned.1.call-start = ((), (), s32[]{:S(2)}) async-start(), calls=%async_computation.1 | async-start | bytes 4194304 | tf_op jit(solution)/shard_map/psum | solution.py:49
  93.3 0.7 copy-start.2
Sparse Core Ops, SparseCore 0:
  55.2 31.9 all-reduce.2
  93.5 57.2 all-reduce.4
where the time goes:
time: 161 us; the launch traced here: 160 us
  waiting for transfers between devices  88.8 us (55%)
  other arithmetic  30.1 us (19%)
  between operations  14.2 us (9%)
  blocking collectives  13.1 us (8%)
  matrix products  12 us (7%)
  local copies, waits for them, and re-layouts  2.12 us (1%)
    psum x1, waiting for transfers between devices, local_block(): projected = lax.psum(partial_out, 'tp')  56.8 us
    psum x1, waiting for transfers between devices, local_block(): totals = lax.psum(combined_in, 'sp')  32.1 us
    pmax x1, blocking collectives, local_block(): global_max = lax.pmax(local_max, 'sp')  13.1 us
    dot_general x1, other arithmetic, local_block(): jnp.einsum('bhd,bhsd->bhs', q_new, k_out, preferred_element_type=jnp.floa...  11.3 us
    dot_general x1, other arithmetic, local_block(): jnp.einsum('bhs,bhsd->bhd', weights.astype(jnp.bfloat16), v_out, preferre...  10.8 us
    unnamed x1, matrix products  6.88 us
    dot_general x1, matrix products, local_block(): jnp.einsum('bhd,hdm->bm', attended, w_out, preferred_element_type=jnp.flo...  5.15 us
  transfers between devices with their start and end apart: 2, of which 2 were waited for; matrix products, arithmetic and copies ran while one was open for 0% of the time, Pallas kernels for 0%

commit v1 on v0

v1 whole, which is shorter than its diff:
```python
import functools
import jax
import jax.numpy as jnp
from jax import lax
from jax.experimental import pallas as pl
from jax.experimental.pallas import tpu as pltpu
from jax.sharding import PartitionSpec as P

F32 = jnp.float32
BF16 = jnp.bfloat16
GROUP = 4


def attend_kernel(x_hbm, len_hbm, gain_hbm, bias_hbm, bqkv_hbm, w_hbm, k_hbm, v_hbm,
                  k_hbm_out, v_hbm_out, acc_out, max_out, sum_out,
                  k_out, v_out, x_buf, len_ref, gain_ref, bias_ref, bqkv_ref, hidden, w_buf, qkv, bias_cols, x_sem, w_sem, k_sem, v_sem, k_out_sem, v_out_sem):
    heads, slots, dim, rows = k_out.shape
    groups = heads // GROUP
    small = [pltpu.make_async_copy(a, b, x_sem.at[n]) for n, (a, b) in enumerate((
        (x_hbm, x_buf), (len_hbm, len_ref), (gain_hbm, gain_ref), (bias_hbm, bias_ref), (bqkv_hbm, bqkv_ref)))]
    for copy in small:
        copy.start()

    def copy_w(g):
        return pltpu.make_async_copy(w_hbm.at[:, pl.ds(g * GROUP, GROUP)], w_buf.at[:, pl.ds(g * GROUP, GROUP)], w_sem.at[g])

    def copy_k(h):
        return pltpu.make_async_copy(k_hbm.at[h], k_out.at[h], k_sem.at[h])

    def copy_v(h):
        return pltpu.make_async_copy(v_hbm.at[h], v_out.at[h], v_sem.at[h])

    def write_k(h):
        return pltpu.make_async_copy(k_out.at[h], k_hbm_out.at[h], k_out_sem.at[h])

    def write_v(h):
        return pltpu.make_async_copy(v_out.at[h], v_hbm_out.at[h], v_out_sem.at[h])

    for g in range(groups):
        copy_w(g).start()
        for h in range(g * GROUP, (g + 1) * GROUP):
            copy_k(h).start()
            copy_v(h).start()

    for copy in small[1:]:
        copy.wait()
    bias_t = bqkv_ref[...].astype(F32).T
    for j in range(3 * heads):
        bias_cols[j] = jnp.broadcast_to(bias_t[:, j:j + 1], (dim, 128))

    small[0].wait()
    chunk = 16

    @pl.loop(0, rows // chunk)
    def _(i):
        at = pl.ds(pl.multiple_of(i * chunk, chunk), chunk)
        x = x_buf[at, :].astype(F32)
        mean = jnp.mean(x, axis=-1, keepdims=True)
        centered = x - mean
        var = jnp.mean(centered * centered, axis=-1, keepdims=True)
        hidden[at, :] = (centered * lax.rsqrt(var + 1e-5) * gain_ref[...] + bias_ref[...]).astype(BF16)

    local_len = len_ref[...] - lax.axis_index('sp') * slots
    head_id = lax.broadcasted_iota(jnp.int32, (heads, 128), 0)
    max_out[...] = jnp.zeros(max_out.shape, F32)
    sum_out[...] = jnp.zeros(sum_out.shape, F32)
    slot = lax.broadcasted_iota(jnp.int32, (slots, 128), 0)

    @pl.loop(0, groups)
    def _(g):
        copy_w(g).wait()
        w = w_buf[:, pl.ds(g * GROUP, GROUP)].reshape(3 * GROUP * dim, w_buf.shape[-1])
        out = lax.dot_general(w, hidden[...], (((1,), (1,)), ((), ())), preferred_element_type=F32)
        qkv[...] = out.reshape(3, GROUP, dim, rows)

        @pl.loop(0, GROUP)
        def _(i):
            h = g * GROUP + i
            copy_k(h).wait()
            copy_v(h).wait()
            for lane in range(rows // 128):
                b = slice(lane * 128, (lane + 1) * 128)
                here = local_len[:, b]
                q_new = (qkv[0, i, :, b] + bias_cols[h]).astype(BF16).astype(F32)
                k_new = (qkv[1, i, :, b] + bias_cols[heads + h]).astype(BF16)
                v_new = (qkv[2, i, :, b] + bias_cols[2 * heads + h]).astype(BF16)
                parts = []
                for s in range(slots):
                    k = jnp.where(here == s, k_new, k_out[h, s, :, b])
                    k_out[h, s, :, b] = k
                    parts.append(jnp.sum(q_new * k.astype(F32), axis=0, keepdims=True))
                scores = jnp.concatenate(parts, axis=0) * dim ** -0.5
                valid = slot <= here
                masked = jnp.where(valid, scores, -1e30)
                top = jnp.max(masked, axis=0, keepdims=True)
                weights = jnp.where(valid, jnp.exp(masked - top), 0.0)
                max_out[:, b] = jnp.where(head_id == h, top, max_out[:, b])
                sum_out[:, b] = jnp.where(head_id == h, jnp.sum(weights, axis=0, keepdims=True), sum_out[:, b])
                weights = weights.astype(BF16).astype(F32)
                acc = jnp.zeros((dim, 128), F32)
                for s in range(slots):
                    v = jnp.where(here == s, v_new, v_out[h, s, :, b])
                    v_out[h, s, :, b] = v
                    acc = acc + weights[s:s + 1, :] * v.astype(F32)
                acc_out[h, :, b] = acc
            write_k(h).start()
            write_v(h).start()

    @pl.loop(0, heads)
    def _(h):
        write_k(h).wait()
        write_v(h).wait()


def attend(x, cache_len, k, v, gain, bias, w, b):
    heads, slots, dim, rows = k.shape
    model = x.shape[1]
    hbm = pl.BlockSpec(memory_space=pltpu.HBM)
    vmem = pl.BlockSpec(memory_space=pltpu.VMEM)
    return pl.pallas_call(
        attend_kernel,
        out_shape=(
            jax.ShapeDtypeStruct(k.shape, BF16), jax.ShapeDtypeStruct(v.shape, BF16),
            jax.ShapeDtypeStruct((heads, dim, rows), F32), jax.ShapeDtypeStruct((heads, rows), F32), jax.ShapeDtypeStruct((heads, rows), F32),
        ),
        in_specs=[hbm] * 8,
        out_specs=(hbm, hbm, vmem, vmem, vmem),
        scratch_shapes=[
            pltpu.VMEM(k.shape, BF16), pltpu.VMEM(v.shape, BF16),
            pltpu.VMEM((rows, model), BF16), pltpu.VMEM((1, rows), jnp.int32),
            pltpu.VMEM((1, model), F32), pltpu.VMEM((1, model), F32), pltpu.VMEM((3 * heads, dim), BF16),
            pltpu.VMEM((rows, model), BF16),
            pltpu.VMEM((3, heads, dim, model), BF16), pltpu.VMEM((3, GROUP, dim, rows), F32),
            pltpu.VMEM((3 * heads, dim, 128), F32),
            pltpu.SemaphoreType.DMA((5,)), pltpu.SemaphoreType.DMA((heads // GROUP,)),
            pltpu.SemaphoreType.DMA((heads,)), pltpu.SemaphoreType.DMA((heads,)),
            pltpu.SemaphoreType.DMA((heads,)), pltpu.SemaphoreType.DMA((heads,)),
        ],
        compiler_params=pltpu.CompilerParams(vmem_limit_bytes=48 << 20),
        name='attend',
    )(x, cache_len.reshape(1, rows), gain.reshape(1, model), bias.reshape(1, model), b, w, k, v)


CHUNKS = 8
PAIRS = 4


def combine_kernel(acc_ref, max_ref, sum_ref, x_hbm, b_hbm, w_hbm, y_ref,
                   core_acc, core_stat, mix, mix_stat, side_acc, side_stat, att, att_t,
                   x_buf, b_buf, w_buf, part, part_in, final, final_core, final_side, final_relay,
                   in_sem, stat_send, stat_recv, core_send, core_recv, side_send, side_recv, att_send, att_recv,
                   part_send, part_recv, fc_send, fc_recv, fs_send, fs_recv, fr_send, fr_recv):
    heads, dim, rows = acc_ref.shape
    tile = 128
    half_heads = heads // 2
    pair = half_heads // PAIRS
    cols = w_buf.shape[1]
    width = cols // CHUNKS
    tp, sp = lax.axis_index('tp'), lax.axis_index('sp')
    core, side = sp % 2, sp // 2
    dp = lax.axis_index('dp')
    core_peer = (dp, tp, sp + 1 - 2 * core)
    side_peer = (dp, tp, (sp + 2) % 4)
    tp_peer = (dp, 1 - tp, sp)

    def remote(src, dst, send, recv, peer):
        return pltpu.make_async_remote_copy(src_ref=src, dst_ref=dst, send_sem=send, recv_sem=recv,
                                            device_id=peer, device_id_type=pl.DeviceIdType.MESH)

    col0 = pl.multiple_of(core * cols, 128)
    row0 = pl.multiple_of(side * tile, 128)
    other_row0 = pl.multiple_of((1 - side) * tile, 128)
    loads = [pltpu.make_async_copy(w_hbm.at[:, pl.ds(col0, cols)], w_buf, in_sem.at[0]),
             pltpu.make_async_copy(x_hbm.at[pl.ds(row0, tile), pl.ds(col0, cols)], x_buf, in_sem.at[1]),
             pltpu.make_async_copy(b_hbm.at[:, pl.ds(col0, cols)], b_buf, in_sem.at[2])]
    for copy in loads:
        copy.start()

    barrier = pltpu.get_barrier_semaphore()
    for peer in (core_peer, side_peer, tp_peer):
        pl.semaphore_signal(barrier, inc=1, device_id=peer, device_id_type=pl.DeviceIdType.MESH)
    pl.semaphore_wait(barrier, 3)

    mine = pl.multiple_of(core * half_heads, half_heads)
    theirs = pl.multiple_of((1 - core) * half_heads, half_heads)
    stat_copies = [remote(src.at[pl.ds(theirs, half_heads)], core_stat.at[n], stat_send.at[n], stat_recv.at[n], core_peer)
                   for n, src in enumerate((max_ref, sum_ref))]
    core_copies = [remote(acc_ref.at[pl.ds(theirs + j * pair, pair)], core_acc.at[pl.ds(j * pair, pair)],
                          core_send.at[j], core_recv.at[j], core_peer) for j in range(PAIRS)]
    for copy in stat_copies + core_copies:
        copy.start()
    for copy in stat_copies:
        copy.wait_recv()
    own_max, own_sum = max_ref[pl.ds(mine, half_heads)], sum_ref[pl.ds(mine, half_heads)]
    top = jnp.maximum(own_max, core_stat[0])
    own_f, core_f = jnp.exp(own_max - top), jnp.exp(core_stat[0] - top)
    mix_stat[0] = top
    mix_stat[1] = own_sum * own_f + core_stat[1] * core_f
    side_stat_copy = remote(mix_stat.at[:, :, pl.ds(other_row0, tile)], side_stat, stat_send.at[2], stat_recv.at[2], side_peer)
    side_stat_copy.start()
    side_copies = [remote(mix.at[pl.ds(j * pair, pair), :, pl.ds(other_row0, tile)], side_acc.at[pl.ds(j * pair, pair)],
                          side_send.at[j], side_recv.at[j], side_peer) for j in range(PAIRS)]
    for j in range(PAIRS):
        core_copies[j].wait_recv()
        for i in range(j * pair, (j + 1) * pair):
            mix[i] = acc_ref[mine + i] * own_f[i:i + 1, :] + core_acc[i] * core_f[i:i + 1, :]
        side_copies[j].start()

    side_stat_copy.wait_recv()
    my_rows = pl.ds(row0, tile)
    own_max = mix_stat[0, :, my_rows]
    top = jnp.maximum(own_max, side_stat[0])
    own_f, side_f = jnp.exp(own_max - top), jnp.exp(side_stat[0] - top)
    total = mix_stat[1, :, my_rows] * own_f + side_stat[1] * side_f
    att_copies = [remote(att.at[pl.ds(mine + j * pair, pair)], att.at[pl.ds(mine + j * pair, pair)],
                         att_send.at[j], att_recv.at[j], core_peer) for j in range(PAIRS)]
    for j in range(PAIRS):
        side_copies[j].wait_recv()
        for i in range(j * pair, (j + 1) * pair):
            blend = mix[i, :, my_rows] * own_f[i:i + 1, :] + side_acc[i] * side_f[i:i + 1, :]
            att[mine + i] = (blend / total[i:i + 1, :]).astype(BF16).astype(F32)
        att_copies[j].start()
    for copy in att_copies:
        copy.wait_recv()
    for copy in loads:
        copy.wait()
    att_t[...] = att[...].reshape(heads * dim, tile).T.astype(BF16)

    part_copies = [remote(part.at[n], part_in.at[n], part_send.at[n], part_recv.at[n], tp_peer) for n in range(CHUNKS)]
    fc_copies = [remote(final.at[n], final_core.at[n], fc_send.at[n], fc_recv.at[n], core_peer) for n in range(CHUNKS)]
    fs_copies = [remote(final.at[n], final_side.at[n], fs_send.at[n], fs_recv.at[n], side_peer) for n in range(CHUNKS)]
    fr_copies = [remote(final_side.at[n], final_relay.at[n], fr_send.at[n], fr_recv.at[n], core_peer) for n in range(CHUNKS)]
    for n in range(CHUNKS):
        part[n] = jnp.dot(att_t[...], w_buf[:, n * width:(n + 1) * width], preferred_element_type=F32)
        part_copies[n].start()

    other_col0 = pl.multiple_of((1 - core) * cols, 128)

    def put(first_row, first_col, n, value):
        y_ref[pl.ds(first_row, tile), pl.ds(pl.multiple_of(first_col + n * width, 128), width)] = value.astype(BF16)

    def finish(n):
        part_copies[n].wait_recv()
        at = slice(n * width, (n + 1) * width)
        out = x_buf[:, at].astype(F32) + (part[n] + part_in[n]) + b_buf[:, at].astype(F32)
        final[n] = out
        fs_copies[n].start()
        fc_copies[n].start()
        put(row0, col0, n, out)

    def take_core(n):
        fc_copies[n].wait_recv()
        put(row0, other_col0, n, final_core[n])

    def take_side(n):
        fs_copies[n].wait_recv()
        fr_copies[n].start()
        put(other_row0, col0, n, final_side[n])

    def take_relay(n):
        fr_copies[n].wait_recv()
        put(other_row0, other_col0, n, final_relay[n])

    for n in range(CHUNKS + 4):
        if n < CHUNKS:
            finish(n)
        if 1 <= n < CHUNKS + 1:
            take_core(n - 1)
        if 2 <= n < CHUNKS + 2:
            take_side(n - 2)
        if 3 <= n < CHUNKS + 3:
            take_relay(n - 3)
    for copy in (stat_copies + [side_stat_copy] + core_copies + side_copies + att_copies
                 + part_copies + fc_copies + fs_copies + fr_copies):
        copy.wait_send()


def combine(acc, top, total, x, b, w):
    heads, dim, rows = acc.shape
    model = x.shape[1]
    cols = model // 2
    half = heads // 2
    tile = 128
    hbm = pl.BlockSpec(memory_space=pltpu.HBM)
    vmem = pl.BlockSpec(memory_space=pltpu.VMEM)
    dma = pltpu.SemaphoreType.DMA
    block = pltpu.VMEM((CHUNKS, tile, cols // CHUNKS), F32)
    return pl.pallas_call(
        combine_kernel,
        out_shape=jax.ShapeDtypeStruct((rows, model), BF16),
        in_specs=[vmem, vmem, vmem, hbm, hbm, hbm],
        out_specs=vmem,
        scratch_shapes=[
            pltpu.VMEM((half, dim, rows), F32), pltpu.VMEM((2, half, rows), F32),
            pltpu.VMEM((half, dim, rows), F32), pltpu.VMEM((2, half, rows), F32),
            pltpu.VMEM((half, dim, tile), F32), pltpu.VMEM((2, half, tile), F32),
            pltpu.VMEM((heads, dim, tile), F32), pltpu.VMEM((tile, heads * dim), BF16),
            pltpu.VMEM((tile, cols), BF16), pltpu.VMEM((1, cols), BF16), pltpu.VMEM((heads * dim, cols), BF16),
            block, block, block, block, block, block,
            dma((3,)), dma((3,)), dma((3,)), dma((PAIRS,)), dma((PAIRS,)), dma((PAIRS,)), dma((PAIRS,)),
            dma((PAIRS,)), dma((PAIRS,)),
        ] + [dma((CHUNKS,))] * 8,
        compiler_params=pltpu.CompilerParams(vmem_limit_bytes=24 << 20, collective_id=0, has_side_effects=True),
        name='combine',
    )(acc, top, total, x, b.reshape(1, model), w.reshape(heads * dim, model))


def solution(mesh):
    cache_spec = P('dp', 'tp', 'sp', None)
    row_spec = P('dp', None)

    def local_block(tok_hidden, cache_len, k_cache, v_cache, ln_gain, ln_bias, w_qkv, b_qkv, w_out, b_out):
        heads, dim = k_cache.shape[1], k_cache.shape[3]
        k_t, v_t = (c.transpose(1, 2, 3, 0) for c in (k_cache, v_cache))
        k_new, v_new, acc, top, total = attend(
            tok_hidden, cache_len, k_t, v_t, ln_gain, ln_bias, w_qkv.transpose(1, 2, 3, 0), b_qkv.reshape(3 * heads, dim))
        y_out = combine(acc, top, total, tok_hidden, b_out, w_out)
        return y_out, k_new.transpose(3, 0, 1, 2), v_new.transpose(3, 0, 1, 2)

    return jax.shard_map(
        local_block,
        mesh=mesh,
        in_specs=(row_spec, P('dp'), cache_spec, cache_spec, P(None), P(None), P(None, None, 'tp', None), P(None, 'tp', None), P('tp', None, None), P(None)),
        out_specs=(row_spec, cache_spec, cache_spec),
        check_vma=False,
    )
```

time: 161 us -> 57.9 us (0.36)
  waiting for transfers between devices: 88.8 us -> 0 us
  Pallas kernels: 0 us -> 51.3 us
  other arithmetic: 30.1 us -> 0 us
  between operations: 14.2 us -> 0.66 us
  blocking collectives: 13.1 us -> 0 us
  matrix products: 12 us -> 0 us
  local copies, waits for them, and re-layouts: 2.12 us -> 5.67 us
    psum x2 -> x0, waiting for transfers between devices: 88.8 us -> none  [the longest x1 56.8 us: local_block(): projected = lax.psum(partial_out, 'tp')]
    pallas_call x0 -> x2, Pallas kernels: none -> 51.3 us  [the longest x1 32.7 us: combine(): pl.pallas_call(combine_kernel, out_shape=jax.ShapeDtypeStruct((rows, mode...]
    dot_general x2 -> x0, other arithmetic: 22 us -> none  [the longest x1 11.3 us: local_block(): jnp.einsum('bhd,bhsd->bhs', q_new, k_out, preferred_element_type=jnp.floa...]
    pmax x1 -> x0, blocking collectives: 13.1 us -> none  [local_block(): global_max = lax.pmax(local_max, 'sp')]
    unnamed x1 -> x0, matrix products: 6.88 us -> none
    dot_general x1 -> x0, matrix products: 5.15 us -> none  [local_block(): jnp.einsum('bhd,hdm->bm', attended, w_out, preferred_element_type=jnp.flo...]
    unnamed x13, local copies, waits for them, and re-layouts: 1.19 us -> 4.98 us
    convert_element_type x4 -> x0, other arithmetic: 3.36 us -> none  [the longest x2 2.87 us: local_block(): y_out = (x_f32 + projected + b_out.astype(jnp.float32)).astype(jnp.bfloat16)]
  transfers between devices with their start and end apart: 2 -> 0, of which waited for: 2 -> 0; matrix products, arithmetic and copies ran while one was open for 0% -> 0% of each run, Pallas kernels for 0% -> 0%
where the time goes in v1:
time: 57.9 us; the launch traced here: 57.6 us
  Pallas kernels  51.3 us (89%)
  local copies, waits for them, and re-layouts  5.67 us (10%)
  between operations  0.66 us (1%)
    pallas_call x1, Pallas kernels, combine(): pl.pallas_call(combine_kernel, out_shape=jax.ShapeDtypeStruct((rows, mode...  32.7 us
    pallas_call x1, Pallas kernels, attend(): pl.pallas_call(attend_kernel, out_shape=(jax.ShapeDtypeStruct(k.shape, BF...  18.6 us
    unnamed x13, local copies, waits for them, and re-layouts  4.98 us

profile of v1, /device:TPU:0, one launch (start us, length us, event | category | flops | bytes accessed | tf_op | source)
XLA Modules:
  0.0 57.6 jit_solution(5197869728913251561)
XLA Ops:
  0.6 0.7 %reshape.28.b_hbm = bf16[1,2048]{1,0:T(2,128)(2,1)S(1)} reshape(bf16[2048]{0:T(1024)(128)(2,1)} %param.19) | data formatting | bytes 8192 | tf_op jit(solution)/shard_map/reshape | solution.py:305
  1.3 0.0 copy-start.1
  1.3 1.2 %copy-done.1 = bf16[256,2048]{1,0:T(8,128)(2,1)S(1)} copy-done((bf16[256,2048]{1,0:T(8,128)(2,1)S(1)}, bf16[256,2048]{1,0:T(8,128)(2,1)}, u32[]{:S(2)}) %copy-start.1) | copy-done | bytes 1048600
  2.5 0.0 copy-start.2
  2.6 0.7 %copy-done.2 = bf16[3,16,64]{2,1,0:T(8,128)(2,1)S(1)} copy-done((bf16[3,16,64]{2,1,0:T(8,128)(2,1)S(1)}, bf16[3,16,64]{2,1,0:T(8,128)(2,1)}, u32[]{:S(2)}) %copy-start.2) | copy-done | bytes 6168
  3.3 0.0 copy-start.3
  3.3 0.7 %copy-done.3 = f32[2048]{0:T(1024)S(1)} copy-done((f32[2048]{0:T(1024)S(1)}, f32[2048]{0:T(1024)}, u32[]{:S(2)}) %copy-start.3) | copy-done | bytes 8216
  4.0 0.0 copy-start.4
  4.0 0.7 %copy-done.4 = f32[2048]{0:T(1024)S(1)} copy-done((f32[2048]{0:T(1024)S(1)}, f32[2048]{0:T(1024)}, u32[]{:S(2)}) %copy-start.4) | copy-done | bytes 8216
  4.7 0.0 copy-start.5
  4.7 0.7 %copy-done.5 = s32[256]{0:T(256)S(1)} copy-done((s32[256]{0:T(256)S(1)}, s32[256]{0:T(256)}, u32[]{:S(2)}) %copy-start.5) | copy-done | bytes 1048
  5.3 0.0 copy-start
  5.3 18.6 %attend.1 = (bf16[16,16,64,256]{3,2,1,0:T(8,128)(2,1)}, bf16[16,16,64,256]{3,2,1,0:T(8,128)(2,1)}, f32[16,64,256]{2,1,0:T(8,128)S(1)}, f32[16,256]{1,0:T(8,128)S(1)}, f32[16,256]{1,0:T(8,128)S(1)}) custom-call(bf16[256,2048]{1,0:T(8,128)(2,1)S(1)} %copy-done.1, s32[1,256]{1,0:T(1,128)S(1)} %bitcast.14, f32[1,2048]{1,0:T(1,128)S(1)} %bitcast.12, ...), custom_call_target="tpu_custom_call" | custom-call | tf_op jit(solution)/shard_map/attend/pallas_call | solution.py:120
  23.9 0.0 copy-done
  23.9 32.7 %combine.1 = bf16[256,2048]{1,0:T(8,128)(2,1)S(1)} custom-call(f32[16,64,256]{2,1,0:T(8,128)S(1)} %get-tuple-element.8.acc_ref, f32[16,256]{1,0:T(8,128)S(1)} %get-tuple-element.9.max_ref, f32[16,256]{1,0:T(8,128)S(1)} %get-tuple-element.10.sum_ref, bf16[256,2048]{1,0:T(8,128)(2,1)S(1)} %copy-done.1, bf16[1,2048]{1,0:T(2,128)(2,1)S(1)} %reshape.28.b_hbm, ...), custom_call_target="tpu_custom_call" | custom-call | tf_op jit(solution)/shard_map/combine/pallas_call | solution.py:288
  56.6 1.0 %copy.14 = bf16[256,2048]{1,0:T(8,128)(2,1)} copy(bf16[256,2048]{1,0:T(8,128)(2,1)S(1)} %combine.1) | data formatting | bytes 2097152
Async XLA Ops:
  1.3 1.2 %copy-start.1 = (bf16[256,2048]{1,0:T(8,128)(2,1)S(1)}, bf16[256,2048]{1,0:T(8,128)(2,1)}, u32[]{:S(2)}) copy-start(bf16[256,2048]{1,0:T(8,128)(2,1)} %x_hbm.3) | copy-start | bytes 3145732
  2.5 0.7 %copy-start.2 = (bf16[3,16,64]{2,1,0:T(8,128)(2,1)S(1)}, bf16[3,16,64]{2,1,0:T(8,128)(2,1)}, u32[]{:S(2)}) copy-start(bf16[3,16,64]{2,1,0:T(8,128)(2,1)} %param.17) | copy-start | bytes 18436
  3.3 0.7 %copy-start.3 = (f32[2048]{0:T(1024)S(1)}, f32[2048]{0:T(1024)}, u32[]{:S(2)}) copy-start(f32[2048]{0:T(1024)} %param.14) | copy-start | bytes 24580
  4.0 0.7 %copy-start.4 = (f32[2048]{0:T(1024)S(1)}, f32[2048]{0:T(1024)}, u32[]{:S(2)}) copy-start(f32[2048]{0:T(1024)} %param.15) | copy-start | bytes 24580
  4.7 0.7 %copy-start.5 = (s32[256]{0:T(256)S(1)}, s32[256]{0:T(256)}, u32[]{:S(2)}) copy-start(s32[256]{0:T(256)} %param.11) | copy-start | bytes 3076
  5.3 18.6 %copy-start = (bf16[16,64,2048]{2,1,0:T(8,128)(2,1)S(1)}, bf16[16,64,2048]{2,1,0:T(8,128)(2,1)}, u32[]{:S(2)}) copy-start(bf16[16,64,2048]{2,1,0:T(8,128)(2,1)} %param.18) | copy-start | bytes 12582916
